TPU v7x, 32 devices: a whole 2x2x4 slice. The times are simulated.
32 devices in a mesh: shard: 32 (over z, y, x, core).
Axes of the slice: x: 2, y: 2, z: 4, core: 2. Of those that a mesh axis runs over, the one named last changes fastest.
Arguments:
- data_t: bfloat16 [8192, 8192], P('shard'), may hold values from -0.125 to 0.125
- labels: int32 [8192], replicated, may hold values from -1 to 1, as said below
- sample_weight: float32 [8192], replicated, may hold values from 0.1 to 4
- w_start: float32 [8192], P('shard'), may hold values from -10 to 10
- alpha_start: float32 [8192], P('shard'), may hold values from 0 to 1
- visit_order: int32 [64, 128], P('shard'), may hold values from 0 to 127, each once within a row
Outputs:
- weights_out: float32 [8192], P('shard')
- alpha_final: float32 [8192], P('shard')
- objective: float32 [], replicated
Inputs may be any that keep to these rules, and one draw needn't show every extreme that they name: `labels`: each label is -1 or +1. `visit_order`: each row is a permutation of 0 to 127.
All inputs are finite; a program needn't handle non-finite values.
Results may differ from a plain program's by a relative error of at most 0.0047.
Values may be sent and summed in bfloat16 or wider, within the bound.
A program may use at most 64 MiB of HBM per device.

v0:
```python
import jax
import jax.numpy as jnp
from jax import lax
from jax.sharding import PartitionSpec as P

GROUP = 16


def sweep_rows(gram_block, label_rows, bound_rows, alpha_rows, margin_rows, visit_rows):
    gram_perm = gram_block[visit_rows][:, visit_rows]
    label_perm = label_rows[visit_rows]
    bound_perm = bound_rows[visit_rows]
    alpha_perm = alpha_rows[visit_rows]
    margin_perm = margin_rows[visit_rows]
    diag_perm = jnp.diagonal(gram_perm) + 1e-06

    def update_group(group_index, state_pair):
        alpha_now, margin_now = state_pair
        first_row = jnp.asarray(group_index * GROUP).astype(jnp.int32)
        group_alpha = lax.dynamic_slice_in_dim(alpha_now, first_row, GROUP)
        group_label = lax.dynamic_slice_in_dim(label_perm, first_row, GROUP)
        group_margin = lax.dynamic_slice_in_dim(margin_now, first_row, GROUP)
        group_diag = lax.dynamic_slice_in_dim(diag_perm, first_row, GROUP)
        group_bound = lax.dynamic_slice_in_dim(bound_perm, first_row, GROUP)
        fresh_alpha = jnp.clip(
            group_alpha + (1.0 - group_label * group_margin) / (2.0 * group_diag), 0.0, group_bound
        )
        change = fresh_alpha - group_alpha
        columns = lax.dynamic_slice_in_dim(gram_perm, first_row, GROUP, 1)
        margin_now = margin_now + 2.0 * jnp.dot(
            columns, group_label * change, precision=lax.Precision.HIGHEST
        )
        alpha_now = lax.dynamic_update_slice_in_dim(alpha_now, fresh_alpha, first_row, 0)
        return (alpha_now, margin_now)

    alpha_perm, margin_perm = lax.fori_loop(
        0, alpha_rows.shape[0] // GROUP, update_group, (alpha_perm, margin_perm)
    )
    return jnp.zeros_like(alpha_rows).at[visit_rows].set(alpha_perm)


def body(data_t, labels, sample_weight, w_start, alpha_start, visit_order):
    device_index = lax.axis_index("shard")
    devices = lax.axis_size("shard")
    local_feat = data_t.shape[0]
    samples = labels.shape[0]
    row_count = alpha_start.shape[0]
    features = local_feat * devices
    label_sign = labels.astype(jnp.float32)
    row_first = device_index * row_count
    own_signs = lax.dynamic_slice_in_dim(label_sign, row_first, row_count)
    own_bound = lax.dynamic_slice_in_dim(sample_weight, row_first, row_count)
    relaid = lax.all_to_all(data_t, "shard", split_axis=1, concat_axis=0, tiled=True)
    start_part = jnp.dot(w_start.astype(jnp.bfloat16), data_t, preferred_element_type=jnp.float32)
    start_margin = lax.psum(start_part, "shard")
    weighted = (
        sample_weight * label_sign * jnp.maximum(0.0, 1.0 - label_sign * start_margin)
    ).astype(jnp.bfloat16)
    ascent = jnp.dot(data_t, weighted, preferred_element_type=jnp.float32)
    column_sq = jnp.einsum("fs,fs->f", data_t, data_t, preferred_element_type=jnp.float32)
    scale_col = column_sq / samples + 1e-06
    stepped = w_start + ascent / (samples * scale_col)
    thresh = 1.0 / (4.0 * features * scale_col)
    primal = stepped - jnp.clip(stepped, -thresh, thresh)
    model_part = jnp.dot(primal.astype(jnp.bfloat16), data_t, preferred_element_type=jnp.float32)
    penalty_part = jnp.sum(jnp.abs(primal)) / (4.0 * features)
    own_margin = lax.psum_scatter(model_part, "shard", scatter_dimension=0, tiled=True)
    loss_part = jnp.sum(own_bound * jnp.square(jnp.maximum(0.0, 1.0 - own_signs * own_margin))) / (
        2.0 * samples
    )
    loss_total, penalty = lax.psum((loss_part, penalty_part), "shard")
    objective = loss_total + penalty
    gram_block = lax.dot_general(
        relaid, relaid, (((0,), (0,)), ((), ())), preferred_element_type=jnp.float32
    )
    block_count = visit_order.shape[0]
    visit_rows = (
        visit_order + (jnp.arange(block_count, dtype=jnp.int32) * visit_order.shape[1])[:, None]
    ).reshape(row_count)
    alpha_zero = own_bound * alpha_start
    alpha_one = sweep_rows(gram_block, own_signs, own_bound, alpha_zero, own_margin, visit_rows)
    change_one = (own_signs * (alpha_one - alpha_zero)).astype(jnp.bfloat16)
    update_part = jnp.dot(relaid, change_one, preferred_element_type=jnp.float32) * (2.0 / devices)
    update_one = lax.psum(update_part, "shard")
    second_margin = own_margin + jnp.dot(
        update_one.astype(jnp.bfloat16), relaid, preferred_element_type=jnp.float32
    )
    alpha_two = sweep_rows(gram_block, own_signs, own_bound, alpha_one, second_margin, visit_rows)
    change_two = (own_signs * (alpha_two - alpha_one)).astype(jnp.bfloat16)
    second_part = jnp.dot(relaid, change_two, preferred_element_type=jnp.float32) * (2.0 / devices)
    feat_first = device_index * local_feat
    update_two = lax.psum(second_part, "shard")
    own_two = lax.dynamic_slice_in_dim(update_two, feat_first, local_feat)
    own_one = lax.dynamic_slice_in_dim(update_one, feat_first, local_feat)
    return (primal + own_one + own_two, alpha_two, objective)


def solution(mesh):
    placed = (P("shard", None), P(), P(), P("shard"), P("shard"), P("shard", None))
    return jax.shard_map(
        body, mesh=mesh, in_specs=placed, out_specs=(P("shard"), P("shard"), P()), check_vma=False
    )
```

profile of v0, /device:TPU:0, one launch (start us, length us, event | category | flops | bytes accessed | tf_op | source)
XLA Modules:
  0.0 315.3 jit_solution(12440864550533348112)
XLA Ops:
  0.6 6.4 %copy.19 = bf16[256,8192]{0,1:T(8,128)(2,1)} copy(bf16[256,8192]{1,0:T(8,128)(2,1)} %param.10) | data formatting | bytes 8388608 | tf_op args[0]
  7.0 6.4 %copy.20 = bf16[256,32,256]{2,0,1:T(8,128)(2,1)} copy(bf16[256,32,256]{0,2,1:T(8,128)(2,1)} %bitcast.48) | data formatting | bytes 8388608 | tf_op jit(solution)/shard_map/all_to_all | solution.py:53
  13.4 7.5 %all-to-all-start = ((bf16[256,32,256]{2,0,1:T(8,128)(2,1)}), bf16[256,32,256]{2,0,1:T(8,128)(2,1)}, u32[]{:S(2)}, u32[]{:S(2)}) async-start(bf16[256,32,256]{2,0,1:T(8,128)(2,1)} %copy.20), calls=%async_computation | async-start | bytes 8388608 | tf_op jit(solution)/shard_map/all_to_all | solution.py:53
  21.0 2.8 fusion.28
  23.8 111.3 %psum.35 = f32[8192]{0:T(1024)S(1)} all-reduce(f32[8192]{0:T(1024)S(1)} %bitcast.53), channel_id=1, replica_groups=mesh['shard'=32] {'shard'}, use_global_device_ids=true, to_apply=%region_0.0 | all-reduce | flops 8192 | bytes 65536 | tf_op jit(solution)/shard_map/psum | solution.py:55
  135.2 3.5 %fusion.29 = f32[1,256]{1,0:T(1,128)S(1)} fusion(bf16[8192,1]{0,1:T(2,128)(2,1)S(1)} %reshape.137, bf16[256,8192]{1,0:T(8,128)(2,1)} %param.10), kind=kOutput, calls=%fused_computation.58 | convolution fusion | flops 4194304 | bytes 4211712 | tf_op jit(solution)/shard_map/dot_general | solution.py:59
  138.8 0.9 fusion.16
  139.7 0.6 abs_reduce_fusion
  140.3 2.8 fusion.30
  143.2 38.2 %all-reduce = f32[8192]{0:T(1024)S(1)} all-reduce(f32[8192]{0:T(1024)S(1)} %bitcast.54), channel_id=2, replica_groups=mesh['shard'=32] {'shard'}, use_global_device_ids=true, to_apply=%region_1.2.clone | all-reduce | flops 8192 | bytes 65536
  181.4 0.7 multiply_reduce_fusion
  182.2 1.9 gather_fusion.3
  184.1 1.9 gather_fusion.2
  186.1 1.9 gather_fusion
  188.1 1.9 gather_fusion.1
  191.3 4.7 %fusion.19 = f32[256,256]{1,0:T(8,128)S(1)} fusion(bf16[256,32,256]{2,0,1:T(8,128)(2,1)} %all-to-all-done), kind=kOutput, calls=%fused_computation.35 | convolution fusion | flops 1073741824 | bytes 4456448 | tf_op jit(solution)/shard_map/dot_general | solution.py:73
  196.1 1.0 gather_fusion.4
  197.2 1.0 gather_fusion.5
  198.3 2.4 gather_fusion.6
  200.7 8.5 %while.30 = (s32[]{:T(128)}, f32[256]{0:T(256)S(1)}, f32[256]{0:T(256)S(1)}, f32[256]{0:T(256)S(1)}, f32[256]{0:T(256)S(1)}, /*index=5*/f32[256]{0:T(256)S(1)}, ...) while((s32[]{:T(128)}, f32[256]{0:T(256)S(1)}, f32[256]{0:T(256)S(1)}, ...), condition=%wide.region_3.4_spmd, body=%wide.region_2.3_spmd.sunk | while | flops 49814 | bytes 145567 | solution.py:36
  200.9 0.2 fusion.57
  201.4 0.2 fusion.57
  202.0 0.2 fusion.57
  202.5 0.2 fusion.57
  203.0 0.2 fusion.57
  203.6 0.2 fusion.57
  204.1 0.2 fusion.57
  204.6 0.2 fusion.57
  205.1 0.2 fusion.57
  205.7 0.2 fusion.57
  206.2 0.2 fusion.57
  206.7 0.2 fusion.57
  207.3 0.2 fusion.57
  207.8 0.2 fusion.57
  208.3 0.2 fusion.57
  208.9 0.2 fusion.57
  209.2 1.4 scatter_custom_fusion
  210.6 1.9 gather_fusion.7
  212.6 3.4 %fusion.31 = f32[1,8192]{1,0:T(1,128)S(1)} fusion(bf16[256,1]{0,1:T(2,128)(2,1)S(1)} %reshape.144, bf16[8192,256]{1,0:T(8,128)(2,1)} %bitcast.14), kind=kOutput, calls=%fused_computation.60 | convolution fusion | flops 4194304 | bytes 4227584 | tf_op jit(solution)/shard_map/dot_general | solution.py:83
  215.9 42.2 %psum.36 = f32[8192]{0:T(1024)S(1)} all-reduce(f32[8192]{0:T(1024)S(1)} %broadcast_multiply_fusion.1), channel_id=1, replica_groups=mesh['shard'=32] {'shard'}, use_global_device_ids=true, to_apply=%region_5.6 | all-reduce | flops 8192 | bytes 65536 | tf_op jit(solution)/shard_map/psum | solution.py:84
  258.2 2.8 fusion.32
  261.0 2.0 gather_fusion.8
  263.0 8.5 %while.31 = (s32[]{:T(128)}, f32[256]{0:T(256)S(1)}, f32[256]{0:T(256)S(1)}, f32[256]{0:T(256)S(1)}, f32[256]{0:T(256)S(1)}, /*index=5*/f32[256]{0:T(256)S(1)}, ...) while((s32[]{:T(128)}, f32[256]{0:T(256)S(1)}, f32[256]{0:T(256)S(1)}, ...), condition=%wide.region_7.8_spmd, body=%wide.region_6.7_spmd.sunk | while | flops 49814 | bytes 145567 | solution.py:36
  263.2 0.2 fusion.61
  271.4 1.4 scatter_custom_fusion.1
  272.9 3.4 %fusion.33 = f32[1,8192]{1,0:T(1,128)S(1)} fusion(bf16[256,1]{0,1:T(2,128)(2,1)S(1)} %reshape.148, bf16[8192,256]{1,0:T(8,128)(2,1)} %bitcast.14), kind=kOutput, calls=%fused_computation.62 | convolution fusion | flops 4194304 | bytes 4227584 | tf_op jit(solution)/shard_map/dot_general | solution.py:90
  276.3 38.4 %all-reduce.1 = (f32[8192]{0:T(1024)S(1)}, f32[]{:T(128)}) all-reduce(f32[8192]{0:T(1024)S(1)} %broadcast_multiply_fusion, f32[]{:T(128)S(6)} %add.173), channel_id=1, replica_groups=mesh['shard'=32] {'shard'}, use_global_device_ids=true, to_apply=%region_9.10 | all-reduce | flops 8193 | bytes 65544 | tf_op jit(solution)/shard_map/psum | solution.py:92
  314.7 0.6 dynamic-slice_add_fusion
  (183 shorter events, 11.8 us)
Async XLA Ops:
  13.4 7.5 %copy-start.6 = (f32[256]{0:T(256)S(1)}, f32[256]{0:T(256)}, u32[]{:S(2)}) copy-start(f32[256]{0:T(256)} %param.13) | copy-start | bytes 3076
  13.4 7.5 %copy-start.1 = (s32[8192]{0:T(1024)S(1)}, s32[8192]{0:T(1024)}, u32[]{:S(2)}) copy-start(s32[8192]{0:T(1024)} %param.11) | copy-start | bytes 98308
  13.4 177.9 %all-to-all-start = ((bf16[256,32,256]{2,0,1:T(8,128)(2,1)}), bf16[256,32,256]{2,0,1:T(8,128)(2,1)}, u32[]{:S(2)}, u32[]{:S(2)}) async-start(bf16[256,32,256]{2,0,1:T(8,128)(2,1)} %copy.20), calls=%async_computation | async-start | bytes 8388608 | tf_op jit(solution)/shard_map/all_to_all | solution.py:53
  20.9 114.3 %copy-start.2 = (f32[8192]{0:T(1024)S(1)}, f32[8192]{0:T(1024)}, u32[]{:S(2)}) copy-start(f32[8192]{0:T(1024)} %param.12) | copy-start | bytes 98308
  135.2 3.6 %copy-start = (bf16[256,8192]{1,0:T(8,128)(2,1)S(1)}, bf16[256,8192]{1,0:T(8,128)(2,1)}, u32[]{:S(2)}) copy-start(bf16[256,8192]{1,0:T(8,128)(2,1)} %param.10) | copy-start | bytes 12582916
  138.8 43.3 %copy-start.5 = (s32[2,128]{1,0:T(2,128)S(1)}, s32[2,128]{1,0:T(2,128)}, u32[]{:S(2)}) copy-start(s32[2,128]{1,0:T(2,128)} %param.15) | copy-start | bytes 3076
  139.7 46.4 %copy-start.3 = (f32[256]{0:T(256)S(1)}, f32[256]{0:T(256)}, u32[]{:S(2)}) copy-start(f32[256]{0:T(256)} %param.14) | copy-start | bytes 3076
  272.9 42.5 %copy-start.4 = (f32[256]{0:T(256)}, f32[256]{0:T(256)S(1)}, u32[]{:S(2)}) copy-start(f32[256]{0:T(256)S(1)} %scatter_custom_fusion.1) | copy-start | bytes 3076
where the time goes:
time: 316 us; the launch traced here: 315 us
  blocking collectives  230 us (73%)
  local copies, waits for them, and re-layouts  32.1 us (10%)
  matrix products  31.5 us (10%)
  other arithmetic  10.4 us (3%)
  starting transfers between devices  7.45 us (2%)
    psum x1, blocking collectives, body(): start_margin = lax.psum(start_part, 'shard')  111 us
    psum x1, blocking collectives, body(): update_one = lax.psum(update_part, 'shard')  42.2 us
    psum x1, blocking collectives, body(): update_two = lax.psum(second_part, 'shard')  38.4 us
    unnamed x1, blocking collectives  38.2 us
    dot_general x32, matrix products, update_group(): jnp.dot(columns, group_label * change, precision=lax.Precision.HIGHEST)  7.97 us
    all_to_all x1, starting transfers between devices, body(): lax.all_to_all(data_t, 'shard', split_axis=1, concat_axis=0, tiled=True)  7.45 us
    unnamed x15, local copies, waits for them, and re-layouts  6.44 us
    all_to_all x1, local copies, waits for them, and re-layouts, body(): lax.all_to_all(data_t, 'shard', split_axis=1, concat_axis=0, tiled=True)  6.41 us
  transfers between devices with their start and end apart: 1, of which 0 were waited for; matrix products, arithmetic and copies ran while one was open for 6% of the time, Pallas kernels for 0%

commit v1 on v0

v1 whole, which is shorter than its diff:
```python
import functools

import jax
import jax.numpy as jnp
from jax import lax
from jax.experimental import pallas as pl
from jax.experimental.pallas import tpu as pltpu
from jax.sharding import PartitionSpec as P

GROUP = 16
ROWS = 16
MESH = pl.DeviceIdType.MESH
F32 = jnp.float32
BF16 = jnp.bfloat16
HIGH = lax.Precision.HIGHEST


def nn(a, b, precision=None):
    return lax.dot_general(a, b, (((1,), (0,)), ((), ())), preferred_element_type=F32, precision=precision)


def nt(a, b, precision=None):
    return lax.dot_general(a, b, (((1,), (1,)), ((), ())), preferred_element_type=F32, precision=precision)


def spread(row):
    return jnp.broadcast_to(row, (ROWS, row.shape[-1])).astype(BF16)


def kernel(
    devices, data_ref, sign_ref, bound_ref, start_ref, frac_ref, visit_ref,
    weight_ref, alpha_ref, objective_ref,
    part0, part1, part2, got0, got1, got2, own0, own1, own2, all0, all1, all2,
    gram, pair_in, pair_sum, gram_in,
    send_sem, recv_sem, pair_send, pair_recv, gram_send, gram_recv,
):
    me = lax.axis_index("shard")
    feats, samples = data_ref.shape
    rows = sign_ref.shape[1]
    blocks, block = visit_ref.shape
    features = feats * devices
    chips = devices // 2
    chip, core = me // 2, me % 2
    partner = 2 * chip + 1 - core

    def columns(k):
        return pl.ds(pl.multiple_of(k * rows, rows), rows)

    def peers(action):
        def step(i, carry):
            action(lax.rem(me + i, devices))
            return carry

        lax.fori_loop(1, devices, step, 0)

    def total_wait(ref, phase):
        view = ref.at[pl.ds(0, devices - 1)]
        return pltpu.make_async_remote_copy(
            src_ref=view, dst_ref=view, send_sem=send_sem.at[phase], recv_sem=recv_sem.at[phase],
            device_id=(partner,), device_id_type=MESH,
        )

    def scatter_start(part, got, phase):
        def send(peer):
            pltpu.make_async_remote_copy(
                src_ref=part.at[peer], dst_ref=got.at[me], send_sem=send_sem.at[phase],
                recv_sem=recv_sem.at[phase], device_id=(peer,), device_id_type=MESH,
            ).start()

        peers(send)
        got[me] = part[me]

    def gather_start(own, everyone, phase):
        def send(peer):
            pltpu.make_async_remote_copy(
                src_ref=own, dst_ref=everyone.at[me], send_sem=send_sem.at[phase],
                recv_sem=recv_sem.at[phase], device_id=(peer,), device_id_type=MESH,
            ).start()

        peers(send)
        everyone[me] = own[...]

    def margin_parts(row, part):
        lhs = spread(row)

        def step(k, carry):
            part[k, 0:1, :] = nn(lhs, data_ref[:, columns(k)])[0:1, :]
            return carry

        lax.fori_loop(0, devices, step, 0, unroll=4)

    def back(everyone):
        def step(k, total):
            return total + nt(spread(everyone[k][0:1, 0:rows]), data_ref[:, columns(k)])

        return lax.fori_loop(0, devices, step, jnp.zeros((ROWS, feats), F32), unroll=4)[0:1, :]

    barrier = pltpu.get_barrier_semaphore()
    peers(lambda peer: pl.semaphore_signal(barrier, inc=1, device_id=(peer,), device_id_type=MESH))

    w_start = start_ref[...]
    sign, bound = sign_ref[...], bound_ref[...]
    margin_parts(w_start, part0)
    pl.semaphore_wait(barrier, devices - 1)
    scatter_start(part0, got0, 0)

    def gram_of(k):
        tile = data_ref[:, columns(k)]
        offset = 0
        for a in range(blocks):
            width = rows - a * block
            piece = lax.dot_general(
                tile[:, a * block:(a + 1) * block], tile[:, a * block:],
                (((0,), (0,)), ((), ())), preferred_element_type=F32,
            )
            gram[k, :, offset:offset + width] = piece.astype(BF16)
            offset += width
        square = tile.astype(F32)
        square = square * square
        part1[k, 1:2, :] = jnp.sum(square, axis=0, keepdims=True)
        return square

    def pair_copy(c):
        return pltpu.make_async_remote_copy(
            src_ref=gram.at[2 * c + 1 - core], dst_ref=pair_in.at[c], send_sem=pair_send.at[c],
            recv_sem=pair_recv.at[c], device_id=(partner,), device_id_type=MESH,
        )

    def gram_step(i, total):
        c = lax.rem(chip + 1 + i, chips)
        square = gram_of(2 * c + 1 - core)
        pair_copy(c).start()
        return total + square + gram_of(2 * c + core)

    square_total = lax.fori_loop(0, chips, gram_step, jnp.zeros((feats, rows), F32))
    column_sq = nt(jnp.ones((8, rows), F32), square_total, HIGH)[0:1, :]

    total_wait(got0, 0).wait_recv()
    margin0 = jnp.sum(got0[...], axis=0)
    own0[...] = bound * sign * jnp.maximum(0.0, 1.0 - sign * margin0)
    gather_start(own0, all0, 0 + 3)

    def gram_copy(c):
        return pltpu.make_async_remote_copy(
            src_ref=pair_sum.at[c], dst_ref=gram_in.at[chip], send_sem=gram_send.at[0],
            recv_sem=gram_recv.at[0], device_id=(2 * c + core,), device_id_type=MESH,
        )

    def merged(c):
        pair_copy(c).wait_recv()
        return (gram[2 * c + core].astype(F32) + pair_in[c].astype(F32)).astype(BF16)

    def merge_step(i, carry):
        c = lax.rem(chip + 1 + i, chips)
        pair_sum[c] = merged(c)
        gram_copy(c).start()
        return carry

    lax.fori_loop(0, chips - 1, merge_step, 0)
    gram_in[chip] = merged(chip)

    total_wait(all0, 3).wait_recv()
    ascent = back(all0)
    scale = column_sq / samples + 1e-06
    stepped = w_start + ascent / (samples * scale)
    thresh = 1.0 / (4.0 * features * scale)
    primal = stepped - jnp.clip(stepped, -thresh, thresh)
    margin_parts(primal, part1)
    scatter_start(part1, got1, 1)

    orders, places = [], []
    for b in range(blocks):
        order = (lax.broadcasted_iota(jnp.int32, (block, block), 0) == visit_ref[b:b + 1, :]).astype(F32)
        orders.append(order)
        places.append(order.T.astype(BF16))

    alpha_zero = bound * frac_ref[...]

    def permute(vectors):
        stacked = jnp.concatenate(list(vectors) + [jnp.zeros((8 - len(vectors), rows), F32)], axis=0)
        return [nn(stacked[:, b * block:(b + 1) * block], orders[b], HIGH) for b in range(blocks)]

    total_wait(got1, 1).wait_recv()
    received = jnp.sum(got1[...], axis=0)
    margin1, diag = received[0:1, :], received[1:2, :]
    loss = jnp.sum(bound * jnp.square(jnp.maximum(0.0, 1.0 - sign * margin1)), axis=1, keepdims=True)
    penalty = jnp.sum(jnp.abs(primal), axis=1, keepdims=True)
    objective_part = loss / (2.0 * samples) + penalty / (4.0 * features)
    permuted = permute((sign, bound, alpha_zero, diag, margin1))
    sign_p = [x[0:1] for x in permuted]
    bound_p = [x[1:2] for x in permuted]
    zero_p = [x[2:3] for x in permuted]
    inverse_p = [0.5 / (x[3:4] + 1e-06) for x in permuted]
    margin_p = [x[4:5] for x in permuted]

    view = gram_in.at[pl.ds(0, chips - 1)]
    gram_wait = pltpu.make_async_remote_copy(
        src_ref=view, dst_ref=view, send_sem=gram_send.at[0], recv_sem=gram_recv.at[0],
        device_id=(partner,), device_id_type=MESH,
    )
    gram_wait.wait_recv()
    full = jnp.sum(gram_in[...].astype(F32), axis=0).astype(BF16)
    blocks_p, offset = {}, 0
    for a in range(blocks):
        for b in range(a, blocks):
            piece = nn(full[:, offset:offset + block], orders[b].astype(BF16)).astype(BF16)
            blocks_p[a, b] = nn(places[a], piece).astype(BF16)
            offset += block

    lane = lax.broadcasted_iota(jnp.int32, (1, block), 1)
    sub = lax.broadcasted_iota(jnp.int32, (ROWS, block), 0)

    def times_gram(delta, piece):
        high = delta.astype(BF16).astype(F32)
        lhs = jnp.where(sub == 0, high, jnp.where(sub == 1, delta - high, 0.0)).astype(BF16)
        return 2.0 * jnp.sum(nn(lhs, piece)[0:8], axis=0, keepdims=True)

    def sweep(alpha, margin):
        result, margin = [], list(margin)
        for b in range(blocks):
            now, m, moved = alpha[b], margin[b], jnp.zeros((1, block), F32)
            for s in range(block // GROUP):
                fresh = jnp.clip(now + (1.0 - sign_p[b] * m) * inverse_p[b], 0.0, bound_p[b])
                mine = (lane >= s * GROUP) & (lane < (s + 1) * GROUP)
                change = jnp.where(mine, fresh - now, 0.0)
                now = jnp.where(mine, fresh, now)
                change = sign_p[b] * change
                moved = moved + change
                if s + 1 < block // GROUP:
                    m = m + times_gram(change, blocks_p[b, b])
            for later in range(b + 1, blocks):
                margin[later] = margin[later] + times_gram(moved, blocks_p[b, later])
            result.append(now)
        return result

    def changes(after, before):
        pieces = []
        for b in range(blocks):
            z = spread(sign_p[b] * (after[b] - before[b]))
            pieces.append(nt(z, orders[b].astype(BF16))[0:1, :])
        return jnp.concatenate(pieces, axis=1)

    one_p = sweep(zero_p, margin_p)
    own1[0:1, 0:rows] = changes(one_p, zero_p)
    own1[0:1, rows:] = jnp.broadcast_to(objective_part, (1, block))
    gather_start(own1, all1, 1 + 3)
    total_wait(all1, 4).wait_recv()
    update_one = back(all1) * (2.0 / devices)
    margin_parts(update_one, part2)
    scatter_start(part2, got2, 2)
    objective_ref[...] = jnp.sum(all1[...], axis=0)[:, rows:]
    total_wait(got2, 2).wait_recv()
    margin2 = margin1 + jnp.sum(got2[...], axis=0)
    margin2_p = [x[0:1] for x in permute((margin2,))]
    two_p = sweep(one_p, margin2_p)
    own2[...] = changes(two_p, one_p)
    gather_start(own2, all2, 2 + 3)
    for b in range(blocks):
        spot = jnp.broadcast_to(two_p[b], (8, block))
        alpha_ref[:, b * block:(b + 1) * block] = nt(spot, orders[b], HIGH)[0:1, :]
    total_wait(all2, 5).wait_recv()
    weight_ref[...] = primal + update_one + back(all2) * (2.0 / devices)

    for phase, ref in enumerate((got0, got1, got2)):
        total_wait(ref, phase).wait_send()
    for phase, ref in enumerate((all0, all1, all2)):
        total_wait(ref, phase + 3).wait_send()
    gram_wait.wait_send()

    def drain(c, carry):
        pair_copy(c).wait_send()
        return carry

    lax.fori_loop(0, chips, drain, 0)


def body(devices, data_t, labels, sample_weight, w_start, alpha_start, visit_order):
    me = lax.axis_index("shard")
    feats = data_t.shape[0]
    rows = alpha_start.shape[0]
    blocks, block = visit_order.shape
    chips = devices // 2
    width = sum(rows - a * block for a in range(blocks))
    sign = lax.dynamic_slice_in_dim(labels, me * rows, rows).astype(F32)[None]
    bound = lax.dynamic_slice_in_dim(sample_weight, me * rows, rows)[None]

    def vectors(height, length):
        return pltpu.VMEM((devices, height, length), F32)

    vmem = pl.BlockSpec(memory_space=pltpu.VMEM)
    weights, alpha, objective = pl.pallas_call(
        functools.partial(kernel, devices),
        name="svm_rounds",
        out_shape=(
            jax.ShapeDtypeStruct((1, feats), F32),
            jax.ShapeDtypeStruct((1, rows), F32),
            jax.ShapeDtypeStruct((1, block), F32),
        ),
        in_specs=[vmem] * 6,
        out_specs=(vmem,) * 3,
        scratch_shapes=[
            vectors(1, rows), vectors(2, rows), vectors(1, rows),
            vectors(1, rows), vectors(2, rows), vectors(1, rows),
            pltpu.VMEM((1, rows), F32), pltpu.VMEM((1, rows + block), F32), pltpu.VMEM((1, rows), F32),
            vectors(1, rows), vectors(1, rows + block), vectors(1, rows),
            pltpu.VMEM((devices, block, width), BF16),
            pltpu.VMEM((chips, block, width), BF16),
            pltpu.VMEM((chips, block, width), BF16),
            pltpu.VMEM((chips, block, width), BF16),
            pltpu.SemaphoreType.DMA((6,)),
            pltpu.SemaphoreType.DMA((6,)),
            pltpu.SemaphoreType.DMA((chips,)),
            pltpu.SemaphoreType.DMA((chips,)),
            pltpu.SemaphoreType.DMA((1,)),
            pltpu.SemaphoreType.DMA((1,)),
        ],
        compiler_params=pltpu.CompilerParams(
            collective_id=0, has_side_effects=True, vmem_limit_bytes=58 * 1024 * 1024
        ),
    )(data_t, sign, bound, w_start[None], alpha_start[None], visit_order)
    return weights[0], alpha[0], objective[0, 0]


def solution(mesh):
    placed = (P("shard", None), P(), P(), P("shard"), P("shard"), P("shard", None))
    return jax.shard_map(
        functools.partial(body, mesh.shape["shard"]), mesh=mesh, in_specs=placed,
        out_specs=(P("shard"), P("shard"), P()), check_vma=False,
    )
```

time: 316 us -> 90 us (0.28)
  blocking collectives: 230 us -> 0 us
  Pallas kernels: 0 us -> 82.2 us
  matrix products: 31.5 us -> 0 us
  local copies, waits for them, and re-layouts: 32.1 us -> 3.76 us
  other arithmetic: 10.4 us -> 1.33 us
  starting transfers between devices: 7.45 us -> 0 us
    psum x3 -> x0, blocking collectives: 192 us -> none  [the longest x1 111 us: body(): start_margin = lax.psum(start_part, 'shard')]
    pallas_call x0 -> x1, Pallas kernels: none -> 82.2 us  [body(): pl.pallas_call(functools.partial(kernel, devices), name='svm_rounds', out...]
    unnamed x1 -> x0, blocking collectives: 38.2 us -> none
    dot_general x39 -> x0, matrix products: 31.5 us -> none  [the longest x32 7.97 us: update_group(): jnp.dot(columns, group_label * change, precision=lax.Precision.HIGHEST)]
    gather x10 -> x0, local copies, waits for them, and re-layouts: 16.1 us -> none  [the longest x2 3.89 us: sweep_rows(): margin_perm = margin_rows[visit_rows]]
    all_to_all x1 -> x0, starting transfers between devices: 7.45 us -> none  [body(): lax.all_to_all(data_t, 'shard', split_axis=1, concat_axis=0, tiled=True)]
    all_to_all x1 -> x0, local copies, waits for them, and re-layouts: 6.41 us -> none  [body(): lax.all_to_all(data_t, 'shard', split_axis=1, concat_axis=0, tiled=True)]
    dynamic_update_slice x32 -> x0, other arithmetic: 5.71 us -> none  [update_group(): lax.dynamic_update_slice_in_dim(alpha_now, fresh_alpha, first_row, 0)]
  transfers between devices with their start and end apart: 1 -> 0, of which waited for: 0 -> 0; matrix products, arithmetic and copies ran while one was open for 6% -> 0% of each run, Pallas kernels for 0% -> 0%
where the time goes in v1:
time: 90 us; the launch traced here: 89.7 us
  Pallas kernels  82.2 us (91%)
  local copies, waits for them, and re-layouts  3.76 us (4%)
  between operations  2.41 us (3%)
  other arithmetic  1.33 us (1%)
    pallas_call x1, Pallas kernels, body(): pl.pallas_call(functools.partial(kernel, devices), name='svm_rounds', out...  82.2 us
    unnamed x2, local copies, waits for them, and re-layouts  2.44 us

profile of v1, /device:TPU:0, one launch (start us, length us, event | category | flops | bytes accessed | tf_op | source)
XLA Modules:
  0.0 89.7 jit_solution(10047600519063403268)
XLA Ops:
  0.6 1.3 %dynamic-slice_convert_fusion = f32[256]{0:T(256)} fusion(s32[8192]{0:T(1024)} %param.7, s32[]{:T(128)S(6)} %select_n.4), kind=kLoop, calls=%fused_computation | loop fusion | flops 256 | bytes 2052 | tf_op jit(solution)/shard_map/convert_element_type | solution.py:284
  2.0 1.3 %dynamic_slice.7 = f32[256]{0:T(256)} dynamic-slice(f32[8192]{0:T(1024)} %param.8, s32[]{:T(128)S(6)} %select_n.4), dynamic_slice_sizes={256} | dynamic-slice | bytes 2052 | tf_op jit(solution)/shard_map/dynamic_slice | solution.py:285
  3.3 82.2 %svm_rounds.1 = (f32[1,256]{1,0:T(1,128)}, f32[1,256]{1,0:T(1,128)}, f32[1,128]{1,0:T(1,128)}) custom-call(bf16[256,8192]{1,0:T(8,128)(2,1)} %data_ref.1, f32[1,256]{1,0:T(1,128)} %bitcast.8, f32[1,256]{1,0:T(1,128)} %bitcast.9, f32[1,256]{1,0:T(1,128)} %bitcast.12, f32[1,256]{1,0:T(1,128)} %bitcast.13, s32[2,128]{1,0:T(2,128)} %visit_ref.1), custom_call_target="tpu_custom_call" | custom-call | tf_op jit(solution)/shard_map/svm_rounds/pallas_call | solution.py:291
  85.5 1.2 %copy.12 = f32[256]{0:T(256)} copy(f32[256]{0:T(256)} %bitcast.11) | data formatting | bytes 2048
  86.7 1.2 %copy.13 = f32[256]{0:T(256)} copy(f32[256]{0:T(256)} %bitcast.10) | data formatting | bytes 2048

commit v2 on v1

--- a/solution.py
+++ b/solution.py
@@ -28,20 +28,21 @@
 
 
 def kernel(
-    devices, data_ref, sign_ref, bound_ref, start_ref, frac_ref, visit_ref,
+    devices, data_ref, label_ref, bound_ref, start_ref, frac_ref, visit_ref,
     weight_ref, alpha_ref, objective_ref,
     part0, part1, part2, got0, got1, got2, own0, own1, own2, all0, all1, all2,
-    gram, pair_in, pair_sum, gram_in,
-    send_sem, recv_sem, pair_send, pair_recv, gram_send, gram_recv,
+    gram, in_a, in_b, in_c, sum_a, sum_b, sum_c, gram_in,
+    send_sem, recv_sem, send_a, recv_a, send_b, recv_b, send_c, recv_c, gram_send, gram_recv,
 ):
     me = lax.axis_index("shard")
     feats, samples = data_ref.shape
-    rows = sign_ref.shape[1]
+    rows = label_ref.shape[2]
     blocks, block = visit_ref.shape
     features = feats * devices
-    chips = devices // 2
-    chip, core = me // 2, me % 2
-    partner = 2 * chip + 1 - core
+    cubes = devices // 8
+    cube = me // 8
+    bit0, bit1, bit2 = me % 2, (me // 2) % 2, (me // 4) % 2
+    partner = me + 1 - 2 * bit0
 
     def columns(k):
         return pl.ds(pl.multiple_of(k * rows, rows), rows)
@@ -99,40 +100,98 @@
     peers(lambda peer: pl.semaphore_signal(barrier, inc=1, device_id=(peer,), device_id_type=MESH))
 
     w_start = start_ref[...]
-    sign, bound = sign_ref[...], bound_ref[...]
+    sign, bound = label_ref[me].astype(F32), bound_ref[me]
     margin_parts(w_start, part0)
     pl.semaphore_wait(barrier, devices - 1)
     scatter_start(part0, got0, 0)
 
+    row_at = lax.broadcasted_iota(jnp.int32, (block, block), 0)
+    lane_at = lax.broadcasted_iota(jnp.int32, (block, block), 1)
+    upper, lower = row_at < lane_at, row_at > lane_at
+
     def gram_of(k):
         tile = data_ref[:, columns(k)]
-        offset = 0
-        for a in range(blocks):
-            width = rows - a * block
-            piece = lax.dot_general(
-                tile[:, a * block:(a + 1) * block], tile[:, a * block:],
-                (((0,), (0,)), ((), ())), preferred_element_type=F32,
-            )
-            gram[k, :, offset:offset + width] = piece.astype(BF16)
-            offset += width
+        first, second = tile[:, :block], tile[:, block:]
+        top = lax.dot_general(first, tile, (((0,), (0,)), ((), ())), preferred_element_type=F32)
+        low = lax.dot_general(second, second, (((0,), (0,)), ((), ())), preferred_element_type=F32)
+        gram[k, :, :block] = jnp.where(upper, top[:, :block], low).astype(BF16)
+        gram[k, :, block:] = top[:, block:].astype(BF16)
         square = tile.astype(F32)
         square = square * square
         part1[k, 1:2, :] = jnp.sum(square, axis=0, keepdims=True)
         return square
 
-    def pair_copy(c):
+    def halving(source, target, index, sends, recvs, peer):
         return pltpu.make_async_remote_copy(
-            src_ref=gram.at[2 * c + 1 - core], dst_ref=pair_in.at[c], send_sem=pair_send.at[c],
-            recv_sem=pair_recv.at[c], device_id=(partner,), device_id_type=MESH,
+            src_ref=source, dst_ref=target.at[index], send_sem=sends.at[index],
+            recv_sem=recvs.at[index], device_id=(peer,), device_id_type=MESH,
         )
 
+    def copy_a(q, j):
+        return halving(gram.at[8 * q + 2 * j + 1 - bit0], in_a, 4 * q + j, send_a, recv_a, partner)
+
+    def copy_b(q, j):
+        return halving(sum_a.at[4 * q + 2 * j + 1 - bit1], in_b, 2 * q + j, send_b, recv_b, me + 2 - 4 * bit1)
+
+    def copy_c(q):
+        return halving(sum_b.at[2 * q + 1 - bit2], in_c, q, send_c, recv_c, me + 4 - 8 * bit2)
+
+    def copy_d(q):
+        return pltpu.make_async_remote_copy(
+            src_ref=sum_c.at[q], dst_ref=gram_in.at[cube], send_sem=gram_send.at[0],
+            recv_sem=gram_recv.at[0], device_id=(me + 8 * (q - cube),), device_id_type=MESH,
+        )
+
+    def added(x, y):
+        return (x.astype(F32) + y.astype(F32)).astype(BF16)
+
+    def turn(i):
+        return lax.rem(cube + 1 + i, cubes)
+
+    def merge_a(i):
+        q = turn(i)
+        for j in range(2):
+            j = (j + 1 + bit2) % 2
+            for side in (1 - bit1, bit1):
+                at = 2 * j + side
+                copy_a(q, at).wait_recv()
+                sum_a[4 * q + at] = added(gram[8 * q + 2 * at + bit0], in_a[4 * q + at])
+            copy_b(q, j).start()
+
+    def merge_b(i):
+        q = turn(i)
+        for j in (1 - bit2, bit2):
+            copy_b(q, j).wait_recv()
+            sum_b[2 * q + j] = added(sum_a[4 * q + 2 * j + bit1], in_b[2 * q + j])
+        copy_c(q).start()
+
+    def merged_c(q):
+        copy_c(q).wait_recv()
+        return added(sum_b[2 * q + bit2], in_c[q])
+
+    def merge_c(i):
+        q = turn(i)
+        sum_c[q] = merged_c(q)
+        copy_d(q).start()
+
+    def loop(count, action):
+        def step(i, carry):
+            action(i)
+            return carry
+
+        lax.fori_loop(0, count, step, 0)
+
     def gram_step(i, total):
-        c = lax.rem(chip + 1 + i, chips)
-        square = gram_of(2 * c + 1 - core)
-        pair_copy(c).start()
-        return total + square + gram_of(2 * c + core)
-
-    square_total = lax.fori_loop(0, chips, gram_step, jnp.zeros((feats, rows), F32))
+        q = turn(i)
+        for j in range(4):
+            total = total + gram_of(8 * q + 2 * j + 1 - bit0)
+            copy_a(q, j).start()
+        for j in range(4):
+            total = total + gram_of(8 * q + 2 * j + bit0)
+        merge_a(i)
+        return total
+
+    square_total = lax.fori_loop(0, cubes, gram_step, jnp.zeros((feats, rows), F32))
     column_sq = nt(jnp.ones((8, rows), F32), square_total, HIGH)[0:1, :]
 
     total_wait(got0, 0).wait_recv()
@@ -140,27 +199,12 @@
     own0[...] = bound * sign * jnp.maximum(0.0, 1.0 - sign * margin0)
     gather_start(own0, all0, 0 + 3)
 
-    def gram_copy(c):
-        return pltpu.make_async_remote_copy(
-            src_ref=pair_sum.at[c], dst_ref=gram_in.at[chip], send_sem=gram_send.at[0],
-            recv_sem=gram_recv.at[0], device_id=(2 * c + core,), device_id_type=MESH,
-        )
-
-    def merged(c):
-        pair_copy(c).wait_recv()
-        return (gram[2 * c + core].astype(F32) + pair_in[c].astype(F32)).astype(BF16)
-
-    def merge_step(i, carry):
-        c = lax.rem(chip + 1 + i, chips)
-        pair_sum[c] = merged(c)
-        gram_copy(c).start()
-        return carry
-
-    lax.fori_loop(0, chips - 1, merge_step, 0)
-    gram_in[chip] = merged(chip)
+    loop(cubes, merge_b)
 
     total_wait(all0, 3).wait_recv()
     ascent = back(all0)
+    loop(cubes - 1, merge_c)
+    gram_in[cube] = merged_c(cube)
     scale = column_sq / samples + 1e-06
     stepped = w_start + ascent / (samples * scale)
     thresh = 1.0 / (4.0 * features * scale)
@@ -193,19 +237,19 @@
     inverse_p = [0.5 / (x[3:4] + 1e-06) for x in permuted]
     margin_p = [x[4:5] for x in permuted]
 
-    view = gram_in.at[pl.ds(0, chips - 1)]
+    view = gram_in.at[pl.ds(0, cubes - 1)]
     gram_wait = pltpu.make_async_remote_copy(
         src_ref=view, dst_ref=view, send_sem=gram_send.at[0], recv_sem=gram_recv.at[0],
         device_id=(partner,), device_id_type=MESH,
     )
     gram_wait.wait_recv()
-    full = jnp.sum(gram_in[...].astype(F32), axis=0).astype(BF16)
-    blocks_p, offset = {}, 0
-    for a in range(blocks):
-        for b in range(a, blocks):
-            piece = nn(full[:, offset:offset + block], orders[b].astype(BF16)).astype(BF16)
-            blocks_p[a, b] = nn(places[a], piece).astype(BF16)
-            offset += block
+    full = jnp.sum(gram_in[...].astype(F32), axis=0)
+    packed, cross = full[:, :block], full[:, block:]
+    above, below = jnp.where(upper, packed, 0.0), jnp.where(lower, packed, 0.0)
+    blocks_p = {}
+    for (a, b), piece in {(0, 0): above + above.T, (0, 1): cross, (1, 1): below + below.T}.items():
+        piece = nn(piece.astype(BF16), orders[b].astype(BF16)).astype(BF16)
+        blocks_p[a, b] = nn(places[a], piece).astype(BF16)
 
     lane = lax.broadcasted_iota(jnp.int32, (1, block), 1)
     sub = lax.broadcasted_iota(jnp.int32, (ROWS, block), 0)
@@ -267,22 +311,29 @@
         total_wait(ref, phase + 3).wait_send()
     gram_wait.wait_send()
 
-    def drain(c, carry):
-        pair_copy(c).wait_send()
-        return carry
-
-    lax.fori_loop(0, chips, drain, 0)
+    def drain(q):
+        for j in range(4):
+            copy_a(q, j).wait_send()
+        for j in range(2):
+            copy_b(q, j).wait_send()
+        copy_c(q).wait_send()
+
+    loop(cubes, drain)
 
 
 def body(devices, data_t, labels, sample_weight, w_start, alpha_start, visit_order):
-    me = lax.axis_index("shard")
     feats = data_t.shape[0]
     rows = alpha_start.shape[0]
     blocks, block = visit_order.shape
-    chips = devices // 2
-    width = sum(rows - a * block for a in range(blocks))
-    sign = lax.dynamic_slice_in_dim(labels, me * rows, rows).astype(F32)[None]
-    bound = lax.dynamic_slice_in_dim(sample_weight, me * rows, rows)[None]
+    cubes = devices // 8
+    labels = labels.reshape(devices, 1, rows)
+    bound = sample_weight.reshape(devices, 1, rows)
+
+    def grams(count):
+        return pltpu.VMEM((count, block, rows), BF16)
+
+    def semaphores(count):
+        return pltpu.SemaphoreType.DMA((count,))
 
     def vectors(height, length):
         return pltpu.VMEM((devices, height, length), F32)
@@ -303,21 +354,16 @@
             vectors(1, rows), vectors(2, rows), vectors(1, rows),
             pltpu.VMEM((1, rows), F32), pltpu.VMEM((1, rows + block), F32), pltpu.VMEM((1, rows), F32),
             vectors(1, rows), vectors(1, rows + block), vectors(1, rows),
-            pltpu.VMEM((devices, block, width), BF16),
-            pltpu.VMEM((chips, block, width), BF16),
-            pltpu.VMEM((chips, block, width), BF16),
-            pltpu.VMEM((chips, block, width), BF16),
-            pltpu.SemaphoreType.DMA((6,)),
-            pltpu.SemaphoreType.DMA((6,)),
-            pltpu.SemaphoreType.DMA((chips,)),
-            pltpu.SemaphoreType.DMA((chips,)),
-            pltpu.SemaphoreType.DMA((1,)),
-            pltpu.SemaphoreType.DMA((1,)),
+            grams(devices), grams(4 * cubes), grams(2 * cubes), grams(cubes),
+            grams(4 * cubes), grams(2 * cubes), grams(cubes), grams(cubes),
+            semaphores(6), semaphores(6), semaphores(4 * cubes), semaphores(4 * cubes),
+            semaphores(2 * cubes), semaphores(2 * cubes), semaphores(cubes), semaphores(cubes),
+            semaphores(1), semaphores(1),
         ],
         compiler_params=pltpu.CompilerParams(
             collective_id=0, has_side_effects=True, vmem_limit_bytes=58 * 1024 * 1024
         ),
-    )(data_t, sign, bound, w_start[None], alpha_start[None], visit_order)
+    )(data_t, labels, bound, w_start[None], alpha_start[None], visit_order)
     return weights[0], alpha[0], objective[0, 0]
 
 

time: 90 us -> 67 us (0.74)
  Pallas kernels: 82.2 us -> 62 us
  other arithmetic: 1.33 us -> 0 us
  local copies, waits for them, and re-layouts: 3.76 us -> 2.44 us
    pallas_call x1, Pallas kernels: 82.2 us -> 62 us  [body(): pl.pallas_call(functools.partial(kernel, devices), name='svm_rounds', out...]
    convert_element_type x1 -> x0, other arithmetic: 1.33 us -> none  [body(): sign = lax.dynamic_slice_in_dim(labels, me * rows, rows).astype(F32)[None]]
    dynamic_slice x1 -> x0, local copies, waits for them, and re-layouts: 1.32 us -> none  [body(): bound = lax.dynamic_slice_in_dim(sample_weight, me * rows, rows)[None]]
where the time goes in v2:
time: 67 us; the launch traced here: 66.8 us
  Pallas kernels  62 us (93%)
  local copies, waits for them, and re-layouts  2.44 us (4%)
  between operations  2.4 us (4%)
    pallas_call x1, Pallas kernels, body(): pl.pallas_call(functools.partial(kernel, devices), name='svm_rounds', out...  62 us
    unnamed x2, local copies, waits for them, and re-layouts  2.44 us

profile of v2, /device:TPU:0, one launch (start us, length us, event | category | flops | bytes accessed | tf_op | source)
XLA Modules:
  0.0 66.8 jit_solution(16427482171526356705)
XLA Ops:
  0.6 62.0 %svm_rounds.1 = (f32[1,256]{1,0:T(1,128)}, f32[1,256]{1,0:T(1,128)}, f32[1,128]{1,0:T(1,128)}) custom-call(bf16[256,8192]{1,0:T(8,128)(2,1)} %data_ref.1, s32[32,1,256]{2,1,0:T(1,128)} %bitcast.8, f32[32,1,256]{2,1,0:T(1,128)} %bitcast.9, f32[1,256]{1,0:T(1,128)} %bitcast.10, f32[1,256]{1,0:T(1,128)} %bitcast.11, s32[2,128]{1,0:T(2,128)} %visit_ref.1), custom_call_target="tpu_custom_call" | custom-call | tf_op jit(solution)/shard_map/svm_rounds/pallas_call | solution.py:342
  62.6 1.2 %copy.12 = f32[256]{0:T(256)} copy(f32[256]{0:T(256)} %bitcast.13) | data formatting | bytes 2048
  63.8 1.2 %copy.13 = f32[256]{0:T(256)} copy(f32[256]{0:T(256)} %bitcast.12) | data formatting | bytes 2048

commit v3 on v2

--- a/solution.py
+++ b/solution.py
@@ -28,14 +28,14 @@
 
 
 def kernel(
-    devices, data_ref, label_ref, bound_ref, start_ref, frac_ref, visit_ref,
+    devices, data_hbm, label_ref, bound_ref, start_ref, frac_ref, visit_ref,
     weight_ref, alpha_ref, objective_ref,
     part0, part1, part2, got0, got1, got2, own0, own1, own2, all0, all1, all2,
-    gram, in_a, in_b, in_c, sum_a, sum_b, sum_c, gram_in,
-    send_sem, recv_sem, send_a, recv_a, send_b, recv_b, send_c, recv_c, gram_send, gram_recv,
+    data_ref, gram, in_a, in_b, in_c, sum_a, sum_b, sum_c, gram_in,
+    load_sem, send_sem, recv_sem, gather_sem, send_a, recv_a, send_b, recv_b, send_c, recv_c, gram_send, gram_recv,
 ):
     me = lax.axis_index("shard")
-    feats, samples = data_ref.shape
+    feats, samples = data_hbm.shape
     rows = label_ref.shape[2]
     blocks, block = visit_ref.shape
     features = feats * devices
@@ -47,63 +47,115 @@
     def columns(k):
         return pl.ds(pl.multiple_of(k * rows, rows), rows)
 
+    def loop(first, last, action):
+        def step(i, carry):
+            action(i)
+            return carry
+
+        lax.fori_loop(first, last, step, 0)
+
+    upward = cube // (cubes // 2)
+
+    def near(i):
+        place = upward * (cubes - 2 - i) + (1 - upward) * i
+        return place + jnp.where(place >= cube, 1, 0)
+
+    def far(i):
+        return near(cubes - 2 - i)
+
+    def mates(action):
+        loop(1, 8, lambda i: action(8 * cube + lax.rem(me + i, 8)))
+
+    def cube_of(q, action):
+        loop(0, 8, lambda j: action(8 * q + j))
+
     def peers(action):
-        def step(i, carry):
-            action(lax.rem(me + i, devices))
-            return carry
-
-        lax.fori_loop(1, devices, step, 0)
+        loop(0, cubes - 1, lambda i: cube_of(far(i), action))
+        mates(action)
+
+    def remote(source, target, send, recv, peer):
+        return pltpu.make_async_remote_copy(
+            src_ref=source, dst_ref=target, send_sem=send, recv_sem=recv,
+            device_id=(peer,), device_id_type=MESH,
+        )
 
     def total_wait(ref, phase):
         view = ref.at[pl.ds(0, devices - 1)]
-        return pltpu.make_async_remote_copy(
-            src_ref=view, dst_ref=view, send_sem=send_sem.at[phase], recv_sem=recv_sem.at[phase],
-            device_id=(partner,), device_id_type=MESH,
-        )
-
-    def scatter_start(part, got, phase):
+        return remote(view, view, send_sem.at[phase], recv_sem.at[phase % 3], partner)
+
+    def scatter_send(part, got, phase):
         def send(peer):
-            pltpu.make_async_remote_copy(
-                src_ref=part.at[peer], dst_ref=got.at[me], send_sem=send_sem.at[phase],
-                recv_sem=recv_sem.at[phase], device_id=(peer,), device_id_type=MESH,
-            ).start()
-
-        peers(send)
+            remote(part.at[peer], got.at[me], send_sem.at[phase], recv_sem.at[phase], peer).start()
+
+        return send
+
+    def gather_start(own, everyone, phase):
+        everyone[me] = own[...]
+        spot = (phase - 3) * cubes + cube
+        peers(lambda peer: remote(own, everyone.at[me], send_sem.at[phase], gather_sem.at[spot], peer).start())
+
+    def part_of(lhs, part, q):
+        for j in range(8):
+            k = 8 * q + j
+            part[k, 0:1, :] = nn(lhs, data_ref[:, columns(k)])[0:1, :]
+
+    def margin_scatter(row, part, got, phase):
+        lhs = spread(row)
+        send = scatter_send(part, got, phase)
+
+        def step(i):
+            q = far(i)
+            part_of(lhs, part, q)
+            cube_of(q, send)
+
+        loop(0, cubes - 1, step)
+        part_of(lhs, part, cube)
+        mates(send)
         got[me] = part[me]
 
-    def gather_start(own, everyone, phase):
-        def send(peer):
-            pltpu.make_async_remote_copy(
-                src_ref=own, dst_ref=everyone.at[me], send_sem=send_sem.at[phase],
-                recv_sem=recv_sem.at[phase], device_id=(peer,), device_id_type=MESH,
-            ).start()
-
-        peers(send)
-        everyone[me] = own[...]
-
-    def margin_parts(row, part):
-        lhs = spread(row)
-
-        def step(k, carry):
-            part[k, 0:1, :] = nn(lhs, data_ref[:, columns(k)])[0:1, :]
-            return carry
-
-        lax.fori_loop(0, devices, step, 0, unroll=4)
-
-    def back(everyone):
-        def step(k, total):
-            return total + nt(spread(everyone[k][0:1, 0:rows]), data_ref[:, columns(k)])
-
-        return lax.fori_loop(0, devices, step, jnp.zeros((ROWS, feats), F32), unroll=4)[0:1, :]
-
+    def back(everyone, phase):
+        def arrival(q, count):
+            view = everyone.at[pl.ds(8 * q, count)]
+            spot = (phase - 3) * cubes + q
+            remote(view, view, send_sem.at[phase], gather_sem.at[spot], partner).wait_recv()
+
+        def cube_sum(q, total):
+            for j in range(8):
+                k = 8 * q + j
+                total = total + nt(spread(everyone[k][0:1, 0:rows]), data_ref[:, columns(k)])
+            return total
+
+        def step(i, total):
+            q = near(i)
+            arrival(q, 8)
+            return cube_sum(q, total)
+
+        arrival(cube, 7)
+        total = cube_sum(cube, jnp.zeros((ROWS, feats), F32))
+        return lax.fori_loop(0, cubes - 1, step, total)[0:1, :]
+
+    def load(q):
+        view = pl.ds(pl.multiple_of(8 * q * rows, rows), 8 * rows)
+        return pltpu.make_async_copy(data_hbm.at[:, view], data_ref.at[:, view], load_sem.at[q])
+
+    loop(0, cubes - 1, lambda i: load(far(i)).start())
+    load(cube).start()
     barrier = pltpu.get_barrier_semaphore()
     peers(lambda peer: pl.semaphore_signal(barrier, inc=1, device_id=(peer,), device_id_type=MESH))
 
     w_start = start_ref[...]
     sign, bound = label_ref[me].astype(F32), bound_ref[me]
-    margin_parts(w_start, part0)
+    start_rows = spread(w_start)
+
+    def first_part(q):
+        load(q).wait()
+        part_of(start_rows, part0, q)
+
+    loop(0, cubes - 1, lambda i: first_part(far(i)))
+    first_part(cube)
     pl.semaphore_wait(barrier, devices - 1)
-    scatter_start(part0, got0, 0)
+    peers(scatter_send(part0, got0, 0))
+    got0[me] = part0[me]
 
     row_at = lax.broadcasted_iota(jnp.int32, (block, block), 0)
     lane_at = lax.broadcasted_iota(jnp.int32, (block, block), 1)
@@ -130,11 +182,20 @@
     def copy_a(q, j):
         return halving(gram.at[8 * q + 2 * j + 1 - bit0], in_a, 4 * q + j, send_a, recv_a, partner)
 
-    def copy_b(q, j):
-        return halving(sum_a.at[4 * q + 2 * j + 1 - bit1], in_b, 2 * q + j, send_b, recv_b, me + 2 - 4 * bit1)
+    def order_of(q):
+        swap = q % 2
+        return (1 - swap) * bit1 + swap * bit2, 1 + swap, (1 - swap) * bit2 + swap * bit1, 2 - swap
+
+    def copy_b(q, t):
+        bit, weight, _, other = order_of(q)
+        return halving(
+            sum_a.at[4 * q + weight * (1 - bit) + other * t], in_b, 2 * q + t, send_b, recv_b,
+            me + 2 * weight * (1 - 2 * bit),
+        )
 
     def copy_c(q):
-        return halving(sum_b.at[2 * q + 1 - bit2], in_c, q, send_c, recv_c, me + 4 - 8 * bit2)
+        _, _, bit, weight = order_of(q)
+        return halving(sum_b.at[2 * q + 1 - bit], in_c, q, send_c, recv_c, me + 2 * weight * (1 - 2 * bit))
 
     def copy_d(q):
         return pltpu.make_async_remote_copy(
@@ -150,36 +211,31 @@
 
     def merge_a(i):
         q = turn(i)
-        for j in range(2):
-            j = (j + 1 + bit2) % 2
-            for side in (1 - bit1, bit1):
-                at = 2 * j + side
+        bit, weight, last, other = order_of(q)
+        for t in (1 - last, last):
+            for side in (1 - bit, bit):
+                at = weight * side + other * t
                 copy_a(q, at).wait_recv()
                 sum_a[4 * q + at] = added(gram[8 * q + 2 * at + bit0], in_a[4 * q + at])
-            copy_b(q, j).start()
+            copy_b(q, t).start()
 
     def merge_b(i):
         q = turn(i)
-        for j in (1 - bit2, bit2):
-            copy_b(q, j).wait_recv()
-            sum_b[2 * q + j] = added(sum_a[4 * q + 2 * j + bit1], in_b[2 * q + j])
+        bit, weight, last, other = order_of(q)
+        for t in (1 - last, last):
+            copy_b(q, t).wait_recv()
+            sum_b[2 * q + t] = added(sum_a[4 * q + weight * bit + other * t], in_b[2 * q + t])
         copy_c(q).start()
 
     def merged_c(q):
+        bit = order_of(q)[2]
         copy_c(q).wait_recv()
-        return added(sum_b[2 * q + bit2], in_c[q])
+        return added(sum_b[2 * q + bit], in_c[q])
 
     def merge_c(i):
         q = turn(i)
         sum_c[q] = merged_c(q)
         copy_d(q).start()
-
-    def loop(count, action):
-        def step(i, carry):
-            action(i)
-            return carry
-
-        lax.fori_loop(0, count, step, 0)
 
     def gram_step(i, total):
         q = turn(i)
@@ -191,26 +247,30 @@
         merge_a(i)
         return total
 
-    square_total = lax.fori_loop(0, cubes, gram_step, jnp.zeros((feats, rows), F32))
-    column_sq = nt(jnp.ones((8, rows), F32), square_total, HIGH)[0:1, :]
-
+    half = cubes // 2
+    square_total = lax.fori_loop(0, half, gram_step, jnp.zeros((feats, rows), F32))
     total_wait(got0, 0).wait_recv()
     margin0 = jnp.sum(got0[...], axis=0)
     own0[...] = bound * sign * jnp.maximum(0.0, 1.0 - sign * margin0)
     gather_start(own0, all0, 0 + 3)
 
-    loop(cubes, merge_b)
-
-    total_wait(all0, 3).wait_recv()
-    ascent = back(all0)
-    loop(cubes - 1, merge_c)
-    gram_in[cube] = merged_c(cube)
+    def late_step(i, total):
+        total = gram_step(i, total)
+        merge_b(i - half)
+        return total
+
+    square_total = lax.fori_loop(half, cubes, late_step, square_total)
+    column_sq = nt(jnp.ones((8, rows), F32), square_total, HIGH)[0:1, :]
+    ascent = back(all0, 3)
+    loop(cubes - half, cubes - 1, merge_b)
     scale = column_sq / samples + 1e-06
     stepped = w_start + ascent / (samples * scale)
     thresh = 1.0 / (4.0 * features * scale)
     primal = stepped - jnp.clip(stepped, -thresh, thresh)
-    margin_parts(primal, part1)
-    scatter_start(part1, got1, 1)
+    margin_scatter(primal, part1, got1, 1)
+    merge_b(cubes - 1)
+    loop(0, cubes - 1, merge_c)
+    gram_in[cube] = merged_c(cube)
 
     orders, places = [], []
     for b in range(blocks):
@@ -288,10 +348,8 @@
     own1[0:1, 0:rows] = changes(one_p, zero_p)
     own1[0:1, rows:] = jnp.broadcast_to(objective_part, (1, block))
     gather_start(own1, all1, 1 + 3)
-    total_wait(all1, 4).wait_recv()
-    update_one = back(all1) * (2.0 / devices)
-    margin_parts(update_one, part2)
-    scatter_start(part2, got2, 2)
+    update_one = back(all1, 4) * (2.0 / devices)
+    margin_scatter(update_one, part2, got2, 2)
     objective_ref[...] = jnp.sum(all1[...], axis=0)[:, rows:]
     total_wait(got2, 2).wait_recv()
     margin2 = margin1 + jnp.sum(got2[...], axis=0)
@@ -302,8 +360,7 @@
     for b in range(blocks):
         spot = jnp.broadcast_to(two_p[b], (8, block))
         alpha_ref[:, b * block:(b + 1) * block] = nt(spot, orders[b], HIGH)[0:1, :]
-    total_wait(all2, 5).wait_recv()
-    weight_ref[...] = primal + update_one + back(all2) * (2.0 / devices)
+    weight_ref[...] = primal + update_one + back(all2, 5) * (2.0 / devices)
 
     for phase, ref in enumerate((got0, got1, got2)):
         total_wait(ref, phase).wait_send()
@@ -318,7 +375,7 @@
             copy_b(q, j).wait_send()
         copy_c(q).wait_send()
 
-    loop(cubes, drain)
+    loop(0, cubes, drain)
 
 
 def body(devices, data_t, labels, sample_weight, w_start, alpha_start, visit_order):
@@ -347,21 +404,21 @@
             jax.ShapeDtypeStruct((1, rows), F32),
             jax.ShapeDtypeStruct((1, block), F32),
         ),
-        in_specs=[vmem] * 6,
+        in_specs=[pl.BlockSpec(memory_space=pl.ANY)] + [vmem] * 5,
         out_specs=(vmem,) * 3,
         scratch_shapes=[
             vectors(1, rows), vectors(2, rows), vectors(1, rows),
             vectors(1, rows), vectors(2, rows), vectors(1, rows),
             pltpu.VMEM((1, rows), F32), pltpu.VMEM((1, rows + block), F32), pltpu.VMEM((1, rows), F32),
             vectors(1, rows), vectors(1, rows + block), vectors(1, rows),
-            grams(devices), grams(4 * cubes), grams(2 * cubes), grams(cubes),
+            pltpu.VMEM(data_t.shape, BF16), grams(devices), grams(4 * cubes), grams(2 * cubes), grams(cubes),
             grams(4 * cubes), grams(2 * cubes), grams(cubes), grams(cubes),
-            semaphores(6), semaphores(6), semaphores(4 * cubes), semaphores(4 * cubes),
+            semaphores(cubes), semaphores(6), semaphores(3), semaphores(3 * cubes), semaphores(4 * cubes), semaphores(4 * cubes),
             semaphores(2 * cubes), semaphores(2 * cubes), semaphores(cubes), semaphores(cubes),
             semaphores(1), semaphores(1),
         ],
         compiler_params=pltpu.CompilerParams(
-            collective_id=0, has_side_effects=True, vmem_limit_bytes=58 * 1024 * 1024
+            collective_id=0, has_side_effects=True, vmem_limit_bytes=63 * 1024 * 1024
         ),
     )(data_t, labels, bound, w_start[None], alpha_start[None], visit_order)
     return weights[0], alpha[0], objective[0, 0]

time: 67 us -> 55.2 us (0.82)
  Pallas kernels: 62 us -> 50.2 us
    pallas_call x1, Pallas kernels: 62 us -> 50.2 us  [body(): pl.pallas_call(functools.partial(kernel, devices), name='svm_rounds', out...]
where the time goes in v3:
time: 55.2 us; the launch traced here: 55 us
  Pallas kernels  50.2 us (91%)
  local copies, waits for them, and re-layouts  2.44 us (4%)
  between operations  2.4 us (4%)
    pallas_call x1, Pallas kernels, body(): pl.pallas_call(functools.partial(kernel, devices), name='svm_rounds', out...  50.2 us
    unnamed x2, local copies, waits for them, and re-layouts  2.44 us

profile of v3, /device:TPU:0, one launch (start us, length us, event | category | flops | bytes accessed | tf_op | source)
XLA Modules:
  0.0 55.0 jit_solution(8588510481823704172)
XLA Ops:
  0.6 50.2 %svm_rounds.1 = (f32[1,256]{1,0:T(1,128)}, f32[1,256]{1,0:T(1,128)}, f32[1,128]{1,0:T(1,128)}) custom-call(bf16[256,8192]{1,0:T(8,128)(2,1)} %data_hbm.1, s32[32,1,256]{2,1,0:T(1,128)} %bitcast.8, f32[32,1,256]{2,1,0:T(1,128)} %bitcast.9, f32[1,256]{1,0:T(1,128)} %bitcast.10, f32[1,256]{1,0:T(1,128)} %bitcast.11, s32[2,128]{1,0:T(2,128)} %visit_ref.1), custom_call_target="tpu_custom_call" | custom-call | tf_op jit(solution)/shard_map/svm_rounds/pallas_call | solution.py:399
  50.8 1.2 %copy.12 = f32[256]{0:T(256)} copy(f32[256]{0:T(256)} %bitcast.13) | data formatting | bytes 2048
  52.0 1.2 %copy.13 = f32[256]{0:T(256)} copy(f32[256]{0:T(256)} %bitcast.12) | data formatting | bytes 2048

commit v4 on v3

--- a/solution.py
+++ b/solution.py
@@ -29,7 +29,7 @@
 
 def kernel(
     devices, data_hbm, label_ref, bound_ref, start_ref, frac_ref, visit_ref,
-    weight_ref, alpha_ref, objective_ref,
+    out_ref,
     part0, part1, part2, got0, got1, got2, own0, own1, own2, all0, all1, all2,
     data_ref, gram, in_a, in_b, in_c, sum_a, sum_b, sum_c, gram_in,
     load_sem, send_sem, recv_sem, gather_sem, send_a, recv_a, send_b, recv_b, send_c, recv_c, gram_send, gram_recv,
@@ -159,7 +159,7 @@
 
     row_at = lax.broadcasted_iota(jnp.int32, (block, block), 0)
     lane_at = lax.broadcasted_iota(jnp.int32, (block, block), 1)
-    upper, lower = row_at < lane_at, row_at > lane_at
+    upper, lower, even = row_at < lane_at, row_at > lane_at, row_at == lane_at
 
     def gram_of(k):
         tile = data_ref[:, columns(k)]
@@ -168,10 +168,10 @@
         low = lax.dot_general(second, second, (((0,), (0,)), ((), ())), preferred_element_type=F32)
         gram[k, :, :block] = jnp.where(upper, top[:, :block], low).astype(BF16)
         gram[k, :, block:] = top[:, block:].astype(BF16)
-        square = tile.astype(F32)
-        square = square * square
-        part1[k, 1:2, :] = jnp.sum(square, axis=0, keepdims=True)
-        return square
+        part1[k, 1:2, :block] = jnp.sum(jnp.where(even, top[:, :block], 0.0), axis=0, keepdims=True)
+        part1[k, 1:2, block:] = jnp.sum(jnp.where(even, low, 0.0), axis=0, keepdims=True)
+        left, right = first.astype(F32), second.astype(F32)
+        return left * left + right * right
 
     def halving(source, target, index, sends, recvs, peer):
         return pltpu.make_async_remote_copy(
@@ -207,7 +207,7 @@
         return (x.astype(F32) + y.astype(F32)).astype(BF16)
 
     def turn(i):
-        return lax.rem(cube + 1 + i, cubes)
+        return jnp.where(i == cubes - 1, cube, far(jnp.minimum(i, cubes - 2)))
 
     def merge_a(i):
         q = turn(i)
@@ -248,7 +248,7 @@
         return total
 
     half = cubes // 2
-    square_total = lax.fori_loop(0, half, gram_step, jnp.zeros((feats, rows), F32))
+    square_total = lax.fori_loop(0, half, gram_step, jnp.zeros((feats, block), F32))
     total_wait(got0, 0).wait_recv()
     margin0 = jnp.sum(got0[...], axis=0)
     own0[...] = bound * sign * jnp.maximum(0.0, 1.0 - sign * margin0)
@@ -260,16 +260,16 @@
         return total
 
     square_total = lax.fori_loop(half, cubes, late_step, square_total)
-    column_sq = nt(jnp.ones((8, rows), F32), square_total, HIGH)[0:1, :]
+    column_sq = nt(jnp.ones((8, block), F32), square_total, HIGH)[0:1, :]
     ascent = back(all0, 3)
-    loop(cubes - half, cubes - 1, merge_b)
+    loop(cubes - half, cubes, merge_b)
+    loop(0, half, merge_c)
     scale = column_sq / samples + 1e-06
     stepped = w_start + ascent / (samples * scale)
     thresh = 1.0 / (4.0 * features * scale)
     primal = stepped - jnp.clip(stepped, -thresh, thresh)
     margin_scatter(primal, part1, got1, 1)
-    merge_b(cubes - 1)
-    loop(0, cubes - 1, merge_c)
+    loop(half, cubes - 1, merge_c)
     gram_in[cube] = merged_c(cube)
 
     orders, places = [], []
@@ -350,7 +350,7 @@
     gather_start(own1, all1, 1 + 3)
     update_one = back(all1, 4) * (2.0 / devices)
     margin_scatter(update_one, part2, got2, 2)
-    objective_ref[...] = jnp.sum(all1[...], axis=0)[:, rows:]
+    out_ref[:, feats + rows:] = jnp.sum(all1[...], axis=0)[:, rows:]
     total_wait(got2, 2).wait_recv()
     margin2 = margin1 + jnp.sum(got2[...], axis=0)
     margin2_p = [x[0:1] for x in permute((margin2,))]
@@ -359,8 +359,8 @@
     gather_start(own2, all2, 2 + 3)
     for b in range(blocks):
         spot = jnp.broadcast_to(two_p[b], (8, block))
-        alpha_ref[:, b * block:(b + 1) * block] = nt(spot, orders[b], HIGH)[0:1, :]
-    weight_ref[...] = primal + update_one + back(all2, 5) * (2.0 / devices)
+        out_ref[:, feats + b * block:feats + (b + 1) * block] = nt(spot, orders[b], HIGH)[0:1, :]
+    out_ref[:, :feats] = primal + update_one + back(all2, 5) * (2.0 / devices)
 
     for phase, ref in enumerate((got0, got1, got2)):
         total_wait(ref, phase).wait_send()
@@ -396,16 +396,12 @@
         return pltpu.VMEM((devices, height, length), F32)
 
     vmem = pl.BlockSpec(memory_space=pltpu.VMEM)
-    weights, alpha, objective = pl.pallas_call(
+    out = pl.pallas_call(
         functools.partial(kernel, devices),
         name="svm_rounds",
-        out_shape=(
-            jax.ShapeDtypeStruct((1, feats), F32),
-            jax.ShapeDtypeStruct((1, rows), F32),
-            jax.ShapeDtypeStruct((1, block), F32),
-        ),
+        out_shape=jax.ShapeDtypeStruct((1, feats + rows + block), F32),
         in_specs=[pl.BlockSpec(memory_space=pl.ANY)] + [vmem] * 5,
-        out_specs=(vmem,) * 3,
+        out_specs=vmem,
         scratch_shapes=[
             vectors(1, rows), vectors(2, rows), vectors(1, rows),
             vectors(1, rows), vectors(2, rows), vectors(1, rows),
@@ -421,7 +417,7 @@
             collective_id=0, has_side_effects=True, vmem_limit_bytes=63 * 1024 * 1024
         ),
     )(data_t, labels, bound, w_start[None], alpha_start[None], visit_order)
-    return weights[0], alpha[0], objective[0, 0]
+    return out[0, :feats], out[0, feats:feats + rows], out[0, feats + rows]
 
 
 def solution(mesh):

time: 55.2 us -> 55.4 us (level)
  Pallas kernels: 50.2 us -> 52.1 us
  between operations: 2.4 us -> 0.64 us
    unnamed x2 -> x0, local copies, waits for them, and re-layouts: 2.44 us -> none
    slice x0 -> x2, local copies, waits for them, and re-layouts: none -> 2.41 us  [body(): return (out[0, :feats], out[0, feats:feats + rows], out[0, feats + rows])]
    pallas_call x1, Pallas kernels: 50.2 us -> 52.1 us  [body(): pl.pallas_call(functools.partial(kernel, devices), name='svm_rounds', out...]
where the time goes in v4:
time: 55.4 us; the launch traced here: 55.2 us
  Pallas kernels  52.1 us (94%)
  local copies, waits for them, and re-layouts  2.41 us (4%)
  between operations  0.64 us (1%)
    pallas_call x1, Pallas kernels, body(): pl.pallas_call(functools.partial(kernel, devices), name='svm_rounds', out...  52.1 us
    slice x2, local copies, waits for them, and re-layouts, body(): return (out[0, :feats], out[0, feats:feats + rows], out[0, feats + rows])  2.41 us

profile of v4, /device:TPU:0, one launch (start us, length us, event | category | flops | bytes accessed | tf_op | source)
XLA Modules:
  0.0 55.2 jit_solution(18249642496917867707)
XLA Ops:
  0.6 52.1 %svm_rounds.1 = f32[1,640]{1,0:T(1,128)} custom-call(bf16[256,8192]{1,0:T(8,128)(2,1)} %data_hbm.1, s32[32,1,256]{2,1,0:T(1,128)} %bitcast.7, f32[32,1,256]{2,1,0:T(1,128)} %bitcast.8, f32[1,256]{1,0:T(1,128)} %bitcast.9, f32[1,256]{1,0:T(1,128)} %bitcast.10, s32[2,128]{1,0:T(2,128)} %visit_ref.1), custom_call_target="tpu_custom_call" | custom-call | tf_op jit(solution)/shard_map/svm_rounds/pallas_call | solution.py:399
  52.8 1.2 %fusion = (f32[1,256]{1,0:T(1,128)}, f32[1,256]{1,0:T(1,128)}) fusion(f32[1,640]{1,0:T(1,128)} %svm_rounds.1), kind=kLoop, calls=%fused_computation | loop fusion | bytes 4096 | tf_op jit(solution)/shard_map/slice | solution.py:420
  54.0 1.2 %slice.11 = f32[1,1]{1,0:T(1,128)} slice(f32[1,640]{1,0:T(1,128)} %svm_rounds.1), slice={[0:1], [512:513]} | slice | bytes 8 | tf_op jit(solution)/shard_map/slice | solution.py:420

commit v5 on v4

--- a/solution.py
+++ b/solution.py
@@ -241,6 +241,7 @@
         q = turn(i)
         for j in range(4):
             total = total + gram_of(8 * q + 2 * j + 1 - bit0)
+        for j in range(4):
             copy_a(q, j).start()
         for j in range(4):
             total = total + gram_of(8 * q + 2 * j + bit0)
@@ -262,14 +263,14 @@
     square_total = lax.fori_loop(half, cubes, late_step, square_total)
     column_sq = nt(jnp.ones((8, block), F32), square_total, HIGH)[0:1, :]
     ascent = back(all0, 3)
-    loop(cubes - half, cubes, merge_b)
-    loop(0, half, merge_c)
+    loop(cubes - half, cubes - 1, merge_b)
     scale = column_sq / samples + 1e-06
     stepped = w_start + ascent / (samples * scale)
     thresh = 1.0 / (4.0 * features * scale)
     primal = stepped - jnp.clip(stepped, -thresh, thresh)
     margin_scatter(primal, part1, got1, 1)
-    loop(half, cubes - 1, merge_c)
+    merge_b(cubes - 1)
+    loop(0, cubes - 1, merge_c)
     gram_in[cube] = merged_c(cube)
 
     orders, places = [], []

time: 55.4 us -> 52.2 us (0.942)
  Pallas kernels: 52.1 us -> 48.9 us
    pallas_call x1, Pallas kernels: 52.1 us -> 48.9 us  [body(): pl.pallas_call(functools.partial(kernel, devices), name='svm_rounds', out...]
where the time goes in v5:
time: 52.2 us; the launch traced here: 51.9 us
  Pallas kernels  48.9 us (94%)
  local copies, waits for them, and re-layouts  2.41 us (5%)
  between operations  0.64 us (1%)
    pallas_call x1, Pallas kernels, body(): pl.pallas_call(functools.partial(kernel, devices), name='svm_rounds', out...  48.9 us
    slice x2, local copies, waits for them, and re-layouts, body(): return (out[0, :feats], out[0, feats:feats + rows], out[0, feats + rows])  2.41 us

profile of v5, /device:TPU:0, one launch (start us, length us, event | category | flops | bytes accessed | tf_op | source)
XLA Modules:
  0.0 51.9 jit_solution(15864742732937940862)
XLA Ops:
  0.6 48.9 %svm_rounds.1 = f32[1,640]{1,0:T(1,128)} custom-call(bf16[256,8192]{1,0:T(8,128)(2,1)} %data_hbm.1, s32[32,1,256]{2,1,0:T(1,128)} %bitcast.7, f32[32,1,256]{2,1,0:T(1,128)} %bitcast.8, f32[1,256]{1,0:T(1,128)} %bitcast.9, f32[1,256]{1,0:T(1,128)} %bitcast.10, s32[2,128]{1,0:T(2,128)} %visit_ref.1), custom_call_target="tpu_custom_call" | custom-call | tf_op jit(solution)/shard_map/svm_rounds/pallas_call | solution.py:400
  49.5 1.2 %fusion = (f32[1,256]{1,0:T(1,128)}, f32[1,256]{1,0:T(1,128)}) fusion(f32[1,640]{1,0:T(1,128)} %svm_rounds.1), kind=kLoop, calls=%fused_computation | loop fusion | bytes 4096 | tf_op jit(solution)/shard_map/slice | solution.py:421
  50.8 1.2 %slice.11 = f32[1,1]{1,0:T(1,128)} slice(f32[1,640]{1,0:T(1,128)} %svm_rounds.1), slice={[0:1], [512:513]} | slice | bytes 8 | tf_op jit(solution)/shard_map/slice | solution.py:421

commit v6 on v5

--- a/solution.py
+++ b/solution.py
@@ -29,7 +29,7 @@
 
 def kernel(
     devices, data_hbm, label_ref, bound_ref, start_ref, frac_ref, visit_ref,
-    out_ref,
+    out_ref, objective_ref,
     part0, part1, part2, got0, got1, got2, own0, own1, own2, all0, all1, all2,
     data_ref, gram, in_a, in_b, in_c, sum_a, sum_b, sum_c, gram_in,
     load_sem, send_sem, recv_sem, gather_sem, send_a, recv_a, send_b, recv_b, send_c, recv_c, gram_send, gram_recv,
@@ -264,13 +264,15 @@
     column_sq = nt(jnp.ones((8, block), F32), square_total, HIGH)[0:1, :]
     ascent = back(all0, 3)
     loop(cubes - half, cubes - 1, merge_b)
+    loop(0, half - 1, merge_c)
     scale = column_sq / samples + 1e-06
     stepped = w_start + ascent / (samples * scale)
     thresh = 1.0 / (4.0 * features * scale)
     primal = stepped - jnp.clip(stepped, -thresh, thresh)
     margin_scatter(primal, part1, got1, 1)
+    loop(half - 1, half, merge_c)
     merge_b(cubes - 1)
-    loop(0, cubes - 1, merge_c)
+    loop(half, cubes - 1, merge_c)
     gram_in[cube] = merged_c(cube)
 
     orders, places = [], []
@@ -351,7 +353,7 @@
     gather_start(own1, all1, 1 + 3)
     update_one = back(all1, 4) * (2.0 / devices)
     margin_scatter(update_one, part2, got2, 2)
-    out_ref[:, feats + rows:] = jnp.sum(all1[...], axis=0)[:, rows:]
+    objective_ref[...] = jnp.sum(all1[...], axis=0)[:, rows:]
     total_wait(got2, 2).wait_recv()
     margin2 = margin1 + jnp.sum(got2[...], axis=0)
     margin2_p = [x[0:1] for x in permute((margin2,))]
@@ -397,12 +399,15 @@
         return pltpu.VMEM((devices, height, length), F32)
 
     vmem = pl.BlockSpec(memory_space=pltpu.VMEM)
-    out = pl.pallas_call(
+    out, objective = pl.pallas_call(
         functools.partial(kernel, devices),
         name="svm_rounds",
-        out_shape=jax.ShapeDtypeStruct((1, feats + rows + block), F32),
+        out_shape=(
+            jax.ShapeDtypeStruct((1, feats + rows), F32),
+            jax.ShapeDtypeStruct((1, block), F32),
+        ),
         in_specs=[pl.BlockSpec(memory_space=pl.ANY)] + [vmem] * 5,
-        out_specs=vmem,
+        out_specs=(vmem, vmem),
         scratch_shapes=[
             vectors(1, rows), vectors(2, rows), vectors(1, rows),
             vectors(1, rows), vectors(2, rows), vectors(1, rows),
@@ -418,7 +423,7 @@
             collective_id=0, has_side_effects=True, vmem_limit_bytes=63 * 1024 * 1024
         ),
     )(data_t, labels, bound, w_start[None], alpha_start[None], visit_order)
-    return out[0, :feats], out[0, feats:feats + rows], out[0, feats + rows]
+    return out[0, :feats], out[0, feats:feats + rows], objective[0, 0]
 
 
 def solution(mesh):

time: 52.2 us -> 52.8 us (1.011)
  between operations: 0.64 us -> 2.4 us
  local copies, waits for them, and re-layouts: 2.41 us -> 1.23 us
    slice x2 -> x1, local copies, waits for them, and re-layouts: 2.41 us -> 1.23 us  [body(): return (out[0, :feats], out[0, feats:feats + rows], objective[0, 0])]
where the time goes in v6:
time: 52.8 us; the launch traced here: 52.6 us
  Pallas kernels  48.9 us (93%)
  between operations  2.4 us (5%)
  local copies, waits for them, and re-layouts  1.23 us (2%)
    pallas_call x1, Pallas kernels, body(): pl.pallas_call(functools.partial(kernel, devices), name='svm_rounds', out...  48.9 us
    slice x1, local copies, waits for them, and re-layouts, body(): return (out[0, :feats], out[0, feats:feats + rows], objective[0, 0])  1.23 us

profile of v6, /device:TPU:0, one launch (start us, length us, event | category | flops | bytes accessed | tf_op | source)
XLA Modules:
  0.0 52.6 jit_solution(10149262963606927669)
XLA Ops:
  0.6 48.9 %svm_rounds.1 = (f32[1,512]{1,0:T(1,128)}, f32[1,128]{1,0:T(1,128)}) custom-call(bf16[256,8192]{1,0:T(8,128)(2,1)} %data_hbm.1, s32[32,1,256]{2,1,0:T(1,128)} %bitcast.8, f32[32,1,256]{2,1,0:T(1,128)} %bitcast.9, f32[1,256]{1,0:T(1,128)} %bitcast.10, f32[1,256]{1,0:T(1,128)} %bitcast.11, s32[2,128]{1,0:T(2,128)} %visit_ref.1), custom_call_target="tpu_custom_call" | custom-call | tf_op jit(solution)/shard_map/svm_rounds/pallas_call | solution.py:402
  49.6 1.2 %fusion = (f32[1,256]{1,0:T(1,128)}, f32[1,256]{1,0:T(1,128)}) fusion(f32[1,512]{1,0:T(1,128)} %get-tuple-element.5), kind=kLoop, calls=%fused_computation | loop fusion | bytes 4096 | tf_op jit(solution)/shard_map/slice | solution.py:426

commit v7 on v6

--- a/solution.py
+++ b/solution.py
@@ -264,15 +264,13 @@
     column_sq = nt(jnp.ones((8, block), F32), square_total, HIGH)[0:1, :]
     ascent = back(all0, 3)
     loop(cubes - half, cubes - 1, merge_b)
-    loop(0, half - 1, merge_c)
     scale = column_sq / samples + 1e-06
     stepped = w_start + ascent / (samples * scale)
     thresh = 1.0 / (4.0 * features * scale)
     primal = stepped - jnp.clip(stepped, -thresh, thresh)
     margin_scatter(primal, part1, got1, 1)
-    loop(half - 1, half, merge_c)
     merge_b(cubes - 1)
-    loop(half, cubes - 1, merge_c)
+    loop(0, cubes - 1, merge_c)
     gram_in[cube] = merged_c(cube)
 
     orders, places = [], []

time: 52.8 us -> 52.7 us (level)
  no operation moved by 1% of the time
where the time goes in v7:
time: 52.7 us; the launch traced here: 52.5 us
  Pallas kernels  48.9 us (93%)
  between operations  2.4 us (5%)
  local copies, waits for them, and re-layouts  1.23 us (2%)
    pallas_call x1, Pallas kernels, body(): pl.pallas_call(functools.partial(kernel, devices), name='svm_rounds', out...  48.9 us
    slice x1, local copies, waits for them, and re-layouts, body(): return (out[0, :feats], out[0, feats:feats + rows], objective[0, 0])  1.23 us

profile of v7, /device:TPU:0, one launch (start us, length us, event | category | flops | bytes accessed | tf_op | source)
XLA Modules:
  0.0 52.5 jit_solution(15989175436798711391)
XLA Ops:
  0.6 48.9 %svm_rounds.1 = (f32[1,512]{1,0:T(1,128)}, f32[1,128]{1,0:T(1,128)}) custom-call(bf16[256,8192]{1,0:T(8,128)(2,1)} %data_hbm.1, s32[32,1,256]{2,1,0:T(1,128)} %bitcast.8, f32[32,1,256]{2,1,0:T(1,128)} %bitcast.9, f32[1,256]{1,0:T(1,128)} %bitcast.10, f32[1,256]{1,0:T(1,128)} %bitcast.11, s32[2,128]{1,0:T(2,128)} %visit_ref.1), custom_call_target="tpu_custom_call" | custom-call | tf_op jit(solution)/shard_map/svm_rounds/pallas_call | solution.py:400
  49.5 1.2 %fusion = (f32[1,256]{1,0:T(1,128)}, f32[1,256]{1,0:T(1,128)}) fusion(f32[1,512]{1,0:T(1,128)} %get-tuple-element.5), kind=kLoop, calls=%fused_computation | loop fusion | bytes 4096 | tf_op jit(solution)/shard_map/slice | solution.py:424
